TPU v7x, 32 devices: a whole 2x2x4 slice. The times are simulated.
32 devices in a mesh: local: 4 (over y, x), dp: 8 (over z, core).
Axes of the slice: x: 2, y: 2, z: 4, core: 2. Of those that a mesh axis runs over, the one named last changes fastest.
Arguments:
- gradient: bfloat16 [32, 72, 7168], P(('local', 'dp')), may hold values from -1.1953125 to 1.1953125
- feedback: bfloat16 [32, 72, 7168], P(('local', 'dp')), may hold values from -0.59765625 to 0.59765625
- basis_in: float32 [7168, 32], replicated, may hold values from -6 to 6
Outputs:
- new_feedback: bfloat16 [32, 72, 7168], P(('local', 'dp'))
- new_basis: float32 [7168, 32], replicated
All inputs are finite; a program needn't handle non-finite values.
Results may differ from a plain program's by a relative error of at most 0.001.
Values sent between devices are 32-bit elements; how exact they have to be, the bound alone decides.
No kernel may reach another device: no remote copies, remote signals or barrier semaphores. Data moves between devices by JAX's collectives and lax.ppermute only.
A program may use at most 64 MiB of HBM per device.

v0:
```python
import jax
import jax.numpy as jnp
from jax import lax
from jax.sharding import PartitionSpec as P

epsilon = 1e-06


def orthonormal(matrix):
    highest = lax.Precision.HIGHEST
    count = matrix.shape[1]
    positions = jnp.arange(count, dtype=jnp.int32)

    def sweep(index, working):
        vector = lax.dynamic_slice_in_dim(working, index, 1, 1)[:, 0]
        vector = vector * lax.rsqrt(jnp.sum(vector * vector) + epsilon)
        projections = jnp.dot(vector, working, precision=highest)
        projections = jnp.where(positions > index, projections, jnp.zeros_like(projections))
        working = working - vector[:, None] * projections[None, :]
        return lax.dynamic_update_slice_in_dim(working, vector[:, None], index, 1)

    return lax.fori_loop(0, count, sweep, matrix)


def body(gradient, feedback, basis_in):
    highest = lax.Precision.HIGHEST
    merged = gradient[0].astype(jnp.float32) + feedback[0].astype(jnp.float32)
    workers = lax.axis_size("local") * lax.axis_size("dp")
    left_term = jnp.dot(merged, basis_in, precision=highest)
    left_sum = lax.psum(left_term, ("local", "dp"))
    left_basis = orthonormal(left_sum)
    right_term = jnp.dot(merged.T, left_basis, precision=highest)
    share_rows = lax.psum_scatter(right_term, "local", scatter_dimension=0, tiled=True)
    share_rows = lax.psum(share_rows, "dp")
    new_basis = lax.all_gather(share_rows, "local", axis=0, tiled=True)
    approx = jnp.dot(left_basis, new_basis.T, precision=highest) / workers
    new_feedback = (merged - approx).astype(jnp.bfloat16)
    return (new_feedback[None], new_basis)


def solution(mesh):
    return jax.shard_map(
        body,
        mesh=mesh,
        in_specs=(P(("local", "dp"), None, None), P(("local", "dp"), None, None), P()),
        out_specs=(P(("local", "dp"), None, None), P()),
        check_vma=False,
    )
```

profile of v0, /device:TPU:0, one launch (start us, length us, event | category | flops | bytes accessed | tf_op | source)
XLA Modules:
  0.0 214.8 jit_solution(16565798836019193358)
XLA Ops:
  7.2 1.1 copy-done
  8.3 3.4 %fusion.8 = f32[72,32]{0,1:T(8,128)S(1)} fusion(f32[7168,32]{0,1:T(8,128)S(1)} %copy-done, bf16[1,72,7168]{2,1,0:T(8,128)(2,1)} %param.6, bf16[1,72,7168]{2,1,0:T(8,128)(2,1)} %param.5), kind=kOutput, calls=%fused_computation.13 | convolution fusion | flops 199729152 | bytes 2991104 | tf_op jit(solution)/shard_map/dot_general | solution.py:29
  11.7 42.1 %psum.14 = f32[72,32]{0,1:T(8,128)S(1)} all-reduce(f32[72,32]{0,1:T(8,128)S(1)} %fusion.8), channel_id=1, replica_groups=mesh['local'=4,'dp'=8] {'local','dp'}, use_global_device_ids=true, to_apply=%region_0.0 | all-reduce | flops 2304 | bytes 18432 | tf_op jit(solution)/shard_map/psum | solution.py:30
  53.8 50.7 %while.14 = (s32[]{:T(128)}, f32[72,32]{0,1:T(8,128)S(1)}, s32[]{:T(128)}, f32[]{:T(128)}, s32[]{:T(128)}) while((s32[]{:T(128)}, f32[72,32]{0,1:T(8,128)S(1)}, s32[]{:T(128)}, f32[]{:T(128)}, s32[]{:T(128)}) %tuple.35), condition=%wide.region_3.4_spmd.clone, body=%wide.region_1.3_spmd.clone.sunk | while | flops 32610 | bytes 30609 | solution.py:22
  57.0 0.6 multiply_reduce_fusion.2
  60.1 0.6 multiply_reduce_fusion.2
  63.3 0.6 multiply_reduce_fusion.2
  68.1 0.6 multiply_reduce_fusion.2
  69.6 0.6 multiply_reduce_fusion.2
  77.6 0.6 multiply_reduce_fusion.2
  79.2 0.6 multiply_reduce_fusion.2
  82.3 0.6 multiply_reduce_fusion.2
  85.5 0.6 multiply_reduce_fusion.2
  88.7 0.6 multiply_reduce_fusion.2
  91.8 0.6 multiply_reduce_fusion.2
  93.4 0.6 multiply_reduce_fusion.2
  95.0 0.6 multiply_reduce_fusion.2
  102.9 0.6 multiply_reduce_fusion.2
  104.5 2.4 %fusion.6 = f32[7168,32]{0,1:T(8,128)} fusion(f32[72,32]{0,1:T(8,128)S(1)} %get-tuple-element.66, bf16[1,72,7168]{2,1,0:T(8,128)(2,1)S(1)} %copy-done.1, bf16[1,72,7168]{2,1,0:T(8,128)(2,1)S(1)} %copy-done.2), kind=kOutput, calls=%fused_computation.11 | convolution fusion | flops 199729152 | bytes 2991104 | tf_op jit(solution)/shard_map/dot_general | solution.py:32
  107.0 27.0 %reduce-scatter.2.cloned.1.call-done = f32[1792,32]{0,1:T(8,128)} async-done(((f32[7168,32]{0,1:T(8,128)}), f32[1792,32]{0,1:T(8,128)}) %reduce-scatter.2.cloned.1.call-update) | async-done | bytes 229392 | tf_op jit(solution)/shard_map/reduce_scatter | solution.py:33
  134.1 55.3 %all-reduce.2.cloned.1.call-done = f32[1792,32]{0,1:T(8,128)} async-done(((f32[1792,32]{0,1:T(8,128)}), f32[1792,32]{0,1:T(8,128)}) %all-reduce.2.cloned.1.call-update) | async-done | bytes 229392 | tf_op jit(solution)/shard_map/psum | solution.py:34
  189.4 14.7 %all_gather.3 = f32[7168,32]{0,1:T(8,128)S(1)} all-gather(f32[1792,32]{0,1:T(8,128)} %all-reduce.2.cloned.1.call-done), channel_id=1, replica_groups=mesh['local'=4,'dp'=8] {'local'}, dimensions={0}, use_global_device_ids=true | all-gather | bytes 1146880 | tf_op jit(solution)/shard_map/all_gather | solution.py:35
  204.1 2.9 %fusion.5 = bf16[1,72,7168]{2,1,0:T(8,128)(2,1)} fusion(f32[72,32]{0,1:T(8,128)S(1)} %get-tuple-element.66, f32[7168,32]{0,1:T(8,128)S(1)} %all_gather.3, bf16[1,72,7168]{2,1,0:T(8,128)(2,1)S(1)} %copy-done.1, bf16[1,72,7168]{2,1,0:T(8,128)(2,1)S(1)} %copy-done.2), kind=kOutput, calls=%fused_computation.10 | convolution fusion | flops 201277440 | bytes 4023296 | tf_op jit(solution)/shard_map/dot_general | solution.py:36
  207.0 0.9 copy.14
  (187 shorter events, 19.5 us)
Async XLA Ops:
  7.2 1.2 copy-start
  7.2 97.3 %copy-start.2 = (bf16[1,72,7168]{2,1,0:T(8,128)(2,1)S(1)}, bf16[1,72,7168]{2,1,0:T(8,128)(2,1)}, u32[]{:S(2)}) copy-start(bf16[1,72,7168]{2,1,0:T(8,128)(2,1)} %param.5) | copy-start | bytes 3096580
  7.2 97.3 %copy-start.1 = (bf16[1,72,7168]{2,1,0:T(8,128)(2,1)S(1)}, bf16[1,72,7168]{2,1,0:T(8,128)(2,1)}, u32[]{:S(2)}) copy-start(bf16[1,72,7168]{2,1,0:T(8,128)(2,1)} %param.6) | copy-start | bytes 3096580
  7.2 126.8 %reduce-scatter.2.cloned.1.call-start = ((), (), s32[]{:S(2)}) async-start(), calls=%async_computation.1 | async-start | bytes 1146880 | tf_op jit(solution)/shard_map/reduce_scatter | solution.py:33
  107.0 82.4 %all-reduce.2.cloned.1.call-start = ((), (), s32[]{:S(2)}) async-start(), calls=%async_computation.2 | async-start | bytes 458752 | tf_op jit(solution)/shard_map/psum | solution.py:34
Sparse Core Ops, SparseCore 0:
  107.1 26.8 reduce-scatter.1
  136.4 52.9 all-reduce.1
where the time goes:
time: 215 us
  waiting for transfers between devices  82.3 us (38%)
  blocking collectives  56.8 us (26%)
  other arithmetic  22.9 us (11%)
  loops' own time  22.8 us (11%)
  between operations  14.1 us (7%)
  matrix products  12.9 us (6%)
  local copies, waits for them, and re-layouts  2.95 us (1%)
    psum x1, waiting for transfers between devices, body(): share_rows = lax.psum(share_rows, 'dp')  55.3 us
    psum x1, blocking collectives, body(): left_sum = lax.psum(left_term, ('local', 'dp'))  42.1 us
    reduce_scatter x1, waiting for transfers between devices, body(): lax.psum_scatter(right_term, 'local', scatter_dimension=0, tiled=True)  27 us
    another operation x1, loops' own time, orthonormal(): return lax.fori_loop(0, count, sweep, matrix)  22.8 us
    reduce_sum x32, other arithmetic, sweep(): vector = vector * lax.rsqrt(jnp.sum(vector * vector) + epsilon)  19.4 us
    all_gather x1, blocking collectives, body(): new_basis = lax.all_gather(share_rows, 'local', axis=0, tiled=True)  14.7 us
  transfers between devices with their start and end apart: 2, of which 2 were waited for; matrix products, arithmetic and copies ran while one was open for 0% of the time, Pallas kernels for 0%

commit v1 on v0

--- a/solution.py
+++ b/solution.py
@@ -32,7 +32,14 @@
     right_term = jnp.dot(merged.T, left_basis, precision=highest)
     share_rows = lax.psum_scatter(right_term, "local", scatter_dimension=0, tiled=True)
     share_rows = lax.psum(share_rows, "dp")
-    new_basis = lax.all_gather(share_rows, "local", axis=0, tiled=True)
+    ring = [share_rows]
+    for hop in range(3):
+        ring.append(lax.ppermute(ring[-1], "local", [(dev, (dev + 1) % 4) for dev in range(4)]))
+    new_basis = jnp.roll(
+        jnp.concatenate(ring[::-1], axis=0),
+        (lax.axis_index("local") + 1) * ring[0].shape[0],
+        axis=0,
+    )
     approx = jnp.dot(left_basis, new_basis.T, precision=highest) / workers
     new_feedback = (merged - approx).astype(jnp.bfloat16)
     return (new_feedback[None], new_basis)

time: 215 us -> 230 us (1.070)
  waiting for transfers between devices: 82.3 us -> 105 us
  blocking collectives: 56.8 us -> 42.1 us
  local copies, waits for them, and re-layouts: 2.95 us -> 7.18 us
    ppermute x0 -> x3, waiting for transfers between devices: none -> 22.8 us  [body(): lax.ppermute(ring[-1], 'local', [(dev, (dev + 1) % 4) for dev in range(4)])]
    all_gather x1 -> x0, blocking collectives: 14.7 us -> none  [body(): new_basis = lax.all_gather(share_rows, 'local', axis=0, tiled=True)]
    unnamed x7 -> x17, local copies, waits for them, and re-layouts: 2.04 us -> 5.94 us
  transfers between devices with their start and end apart: 2 -> 5, of which waited for: 2 -> 5; matrix products, arithmetic and copies ran while one was open for 0% -> 0% of each run, Pallas kernels for 0% -> 0%
where the time goes in v1:
time: 230 us; the launch traced here: 229 us
  waiting for transfers between devices  105 us (46%)
  blocking collectives  42.1 us (18%)
  other arithmetic  22.9 us (10%)
  loops' own time  22.8 us (10%)
  between operations  14.1 us (6%)
  matrix products  12.9 us (6%)
  local copies, waits for them, and re-layouts  7.18 us (3%)
    psum x1, waiting for transfers between devices, body(): share_rows = lax.psum(share_rows, 'dp')  55.3 us
    psum x1, blocking collectives, body(): left_sum = lax.psum(left_term, ('local', 'dp'))  42.1 us
    reduce_scatter x1, waiting for transfers between devices, body(): lax.psum_scatter(right_term, 'local', scatter_dimension=0, tiled=True)  27 us
    another operation x1, loops' own time, orthonormal(): return lax.fori_loop(0, count, sweep, matrix)  22.8 us
    ppermute x3, waiting for transfers between devices, body(): lax.ppermute(ring[-1], 'local', [(dev, (dev + 1) % 4) for dev in range(4)])  22.8 us
    reduce_sum x32, other arithmetic, sweep(): vector = vector * lax.rsqrt(jnp.sum(vector * vector) + epsilon)  19.4 us
    unnamed x17, local copies, waits for them, and re-layouts  5.94 us
  transfers between devices with their start and end apart: 5, of which 5 were waited for; matrix products, arithmetic and copies ran while one was open for 0% of the time, Pallas kernels for 0%

profile of v1, /device:TPU:0, one launch (start us, length us, event | category | flops | bytes accessed | tf_op | source)
XLA Modules:
  0.0 229.2 jit_solution(12756359186477263850)
XLA Ops:
  7.2 1.1 copy-done
  8.3 3.4 %fusion.8 = f32[72,32]{0,1:T(8,128)S(1)} fusion(f32[7168,32]{0,1:T(8,128)S(1)} %copy-done, bf16[1,72,7168]{2,1,0:T(8,128)(2,1)} %param.6, bf16[1,72,7168]{2,1,0:T(8,128)(2,1)} %param.5), kind=kOutput, calls=%fused_computation.13 | convolution fusion | flops 199729152 | bytes 2991104 | tf_op jit(solution)/shard_map/dot_general | solution.py:29
  11.7 42.1 %psum.14 = f32[72,32]{0,1:T(8,128)S(1)} all-reduce(f32[72,32]{0,1:T(8,128)S(1)} %fusion.8), channel_id=1, replica_groups=mesh['local'=4,'dp'=8] {'local','dp'}, use_global_device_ids=true, to_apply=%region_0.0 | all-reduce | flops 2304 | bytes 18432 | tf_op jit(solution)/shard_map/psum | solution.py:30
  53.8 50.7 %while.14 = (s32[]{:T(128)}, f32[72,32]{0,1:T(8,128)S(1)}, s32[]{:T(128)}, f32[]{:T(128)}, s32[]{:T(128)}) while((s32[]{:T(128)}, f32[72,32]{0,1:T(8,128)S(1)}, s32[]{:T(128)}, f32[]{:T(128)}, s32[]{:T(128)}) %tuple.35), condition=%wide.region_3.4_spmd.clone, body=%wide.region_1.3_spmd.clone.sunk | while | flops 32610 | bytes 30609 | solution.py:22
  57.0 0.6 multiply_reduce_fusion.2
  60.1 0.6 multiply_reduce_fusion.2
  63.3 0.6 multiply_reduce_fusion.2
  66.5 0.6 multiply_reduce_fusion.2
  68.1 0.6 multiply_reduce_fusion.2
  74.4 0.6 multiply_reduce_fusion.2
  76.0 0.6 multiply_reduce_fusion.2
  104.5 2.4 %fusion.6 = f32[7168,32]{0,1:T(8,128)} fusion(f32[72,32]{0,1:T(8,128)S(1)} %get-tuple-element.66, bf16[1,72,7168]{2,1,0:T(8,128)(2,1)S(1)} %copy-done.1, bf16[1,72,7168]{2,1,0:T(8,128)(2,1)S(1)} %copy-done.2), kind=kOutput, calls=%fused_computation.11 | convolution fusion | flops 199729152 | bytes 2991104 | tf_op jit(solution)/shard_map/dot_general | solution.py:32
  107.0 27.0 %reduce-scatter.2.cloned.1.call-done = f32[1792,32]{0,1:T(8,128)} async-done(((f32[7168,32]{0,1:T(8,128)}), f32[1792,32]{0,1:T(8,128)}) %reduce-scatter.2.cloned.1.call-update) | async-done | bytes 229392 | tf_op jit(solution)/shard_map/reduce_scatter | solution.py:33
  134.1 55.3 %all-reduce.2.cloned.1.call-done = f32[1792,32]{0,1:T(8,128)} async-done(((f32[1792,32]{0,1:T(8,128)}), f32[1792,32]{0,1:T(8,128)}) %all-reduce.2.cloned.1.call-update) | async-done | bytes 229392 | tf_op jit(solution)/shard_map/psum | solution.py:34
  189.4 1.5 collective-permute-start
  190.9 7.7 %collective-permute-done = f32[1792,32]{0,1:T(8,128)S(1)} collective-permute-done((f32[1792,32]{0,1:T(8,128)}, f32[1792,32]{0,1:T(8,128)S(1)}, u32[]{:S(2)}, u32[]{:S(2)}) %collective-permute-start) | collective-permute-done | bytes 229408 | tf_op jit(solution)/shard_map/ppermute | solution.py:37
  199.1 7.6 %collective-permute-done.1 = f32[1792,32]{0,1:T(8,128)} collective-permute-done((f32[1792,32]{0,1:T(8,128)S(1)}, f32[1792,32]{0,1:T(8,128)}, u32[]{:S(2)}, u32[]{:S(2)}) %collective-permute-start.1) | collective-permute-done | bytes 229408 | tf_op jit(solution)/shard_map/ppermute | solution.py:37
  206.7 7.5 %collective-permute-done.2 = f32[1792,32]{0,1:T(8,128)} collective-permute-done((f32[1792,32]{0,1:T(8,128)}, f32[1792,32]{0,1:T(8,128)}, u32[]{:S(2)}, u32[]{:S(2)}) %collective-permute-start.2) | collective-permute-done | bytes 229408 | tf_op jit(solution)/shard_map/ppermute | solution.py:37
  214.2 1.0 constant_dynamic-update-slice_fusion.7
  215.2 1.0 constant_dynamic-update-slice_fusion.6
  216.1 1.0 constant_dynamic-update-slice_fusion.4
  217.1 1.0 constant_dynamic-update-slice_fusion.3
  218.1 1.0 constant_dynamic-update-slice_fusion.2
  219.4 3.0 %fusion.5 = bf16[1,72,7168]{2,1,0:T(8,128)(2,1)} fusion(f32[72,32]{0,1:T(8,128)S(1)} %get-tuple-element.66, f32[7168,32]{0,1:T(8,128)S(1)} %constant_dynamic-slice_fusion.1, bf16[1,72,7168]{2,1,0:T(8,128)(2,1)S(1)} %copy-done.1, bf16[1,72,7168]{2,1,0:T(8,128)(2,1)S(1)} %copy-done.2), kind=kOutput, calls=%fused_computation.10 | convolution fusion | flops 201277440 | bytes 4023296 | tf_op jit(solution)/shard_map/dot_general | solution.py:43
  (204 shorter events, 24.7 us)
Async XLA Ops:
  7.2 1.2 copy-start
  7.2 97.3 %copy-start.2 = (bf16[1,72,7168]{2,1,0:T(8,128)(2,1)S(1)}, bf16[1,72,7168]{2,1,0:T(8,128)(2,1)}, u32[]{:S(2)}) copy-start(bf16[1,72,7168]{2,1,0:T(8,128)(2,1)} %param.5) | copy-start | bytes 3096580
  7.2 97.3 %copy-start.1 = (bf16[1,72,7168]{2,1,0:T(8,128)(2,1)S(1)}, bf16[1,72,7168]{2,1,0:T(8,128)(2,1)}, u32[]{:S(2)}) copy-start(bf16[1,72,7168]{2,1,0:T(8,128)(2,1)} %param.6) | copy-start | bytes 3096580
  7.2 126.8 %reduce-scatter.2.cloned.1.call-start = ((), (), s32[]{:S(2)}) async-start(), calls=%async_computation.1 | async-start | bytes 1146880 | tf_op jit(solution)/shard_map/reduce_scatter | solution.py:33
  107.0 82.4 %all-reduce.2.cloned.1.call-start = ((), (), s32[]{:S(2)}) async-start(), calls=%async_computation.2 | async-start | bytes 458752 | tf_op jit(solution)/shard_map/psum | solution.py:34
  189.4 29.7 %copy-start.4 = (f32[1792,32]{0,1:T(8,128)S(1)}, f32[1792,32]{0,1:T(8,128)}, u32[]{:S(2)}) copy-start(f32[1792,32]{0,1:T(8,128)} %all-reduce.2.cloned.1.call-done) | copy-start | bytes 688132
  189.4 9.1 %collective-permute-start = (f32[1792,32]{0,1:T(8,128)}, f32[1792,32]{0,1:T(8,128)S(1)}, u32[]{:S(2)}, u32[]{:S(2)}) collective-permute-start(f32[1792,32]{0,1:T(8,128)} %all-reduce.2.cloned.1.call-done), channel_id=1, source_target_pairs={{0,8},{8,16},{16,24},{24,0},{1,9},{9,17},{17,25},{25,1},{2,10},{10... | collective-permute-start | bytes 688136 | tf_op jit(solution)/shard_map/ppermute | solution.py:37
  198.5 8.2 %collective-permute-start.1 = (f32[1792,32]{0,1:T(8,128)S(1)}, f32[1792,32]{0,1:T(8,128)}, u32[]{:S(2)}, u32[]{:S(2)}) collective-permute-start(f32[1792,32]{0,1:T(8,128)S(1)} %collective-permute-done), channel_id=1, source_target_pairs={{0,8},{8,16},{16,24},{24,0},{1,9},{9,17},{17,25},{25,1},{2,10},{10... | collective-permute-start | bytes 688136 | tf_op jit(solution)/shard_map/ppermute | solution.py:37
  206.7 7.5 %collective-permute-start.2 = (f32[1792,32]{0,1:T(8,128)}, f32[1792,32]{0,1:T(8,128)}, u32[]{:S(2)}, u32[]{:S(2)}) collective-permute-start(f32[1792,32]{0,1:T(8,128)} %collective-permute-done.1), channel_id=1, source_target_pairs={{0,8},{8,16},{16,24},{24,0},{1,9},{9,17},{17,25},{25,1},{2,10},{10... | collective-permute-start | bytes 688136 | tf_op jit(solution)/shard_map/ppermute | solution.py:37
  219.4 3.0 %copy-start.3 = (f32[7168,32]{0,1:T(8,128)}, f32[7168,32]{0,1:T(8,128)S(1)}, u32[]{:S(2)}) copy-start(f32[7168,32]{0,1:T(8,128)S(1)} %constant_dynamic-slice_fusion.1) | copy-start | bytes 2752516
Sparse Core Ops, SparseCore 0:
  107.1 26.8 reduce-scatter.1
  136.4 52.9 all-reduce.1

commit v2 on v0

--- a/solution.py
+++ b/solution.py
@@ -31,7 +31,7 @@
     left_basis = orthonormal(left_sum)
     right_term = jnp.dot(merged.T, left_basis, precision=highest)
     share_rows = lax.psum_scatter(right_term, "local", scatter_dimension=0, tiled=True)
-    share_rows = lax.psum(share_rows, "dp")
+    share_rows = jnp.sum(lax.all_gather(share_rows, "dp"), axis=0)
     new_basis = lax.all_gather(share_rows, "local", axis=0, tiled=True)
     approx = jnp.dot(left_basis, new_basis.T, precision=highest) / workers
     new_feedback = (merged - approx).astype(jnp.bfloat16)

time: 215 us -> 190 us (0.88)
  waiting for transfers between devices: 82.3 us -> 55.6 us
    psum x1 -> x0, waiting for transfers between devices: 55.3 us -> none  [body(): share_rows = lax.psum(share_rows, 'dp')]
    all_gather x0 -> x1, waiting for transfers between devices: none -> 28.6 us  [body(): share_rows = jnp.sum(lax.all_gather(share_rows, 'dp'), axis=0)]
where the time goes in v2:
time: 190 us
  waiting for transfers between devices  55.6 us (29%)
  blocking collectives  55.3 us (29%)
  loops' own time  23.3 us (12%)
  other arithmetic  23.2 us (12%)
  between operations  14.1 us (7%)
  matrix products  12.9 us (7%)
  local copies, waits for them, and re-layouts  5.07 us (3%)
    psum x1, blocking collectives, body(): left_sum = lax.psum(left_term, ('local', 'dp'))  42.1 us
    all_gather x1, waiting for transfers between devices, body(): share_rows = jnp.sum(lax.all_gather(share_rows, 'dp'), axis=0)  28.6 us
    reduce_scatter x1, waiting for transfers between devices, body(): lax.psum_scatter(right_term, 'local', scatter_dimension=0, tiled=True)  27 us
    another operation x1, loops' own time, orthonormal(): return lax.fori_loop(0, count, sweep, matrix)  23.3 us
    reduce_sum x32, other arithmetic, sweep(): vector = vector * lax.rsqrt(jnp.sum(vector * vector) + epsilon)  19.4 us
    all_gather x1, blocking collectives, body(): new_basis = lax.all_gather(share_rows, 'local', axis=0, tiled=True)  13.2 us
    dot_general x32, matrix products, sweep(): projections = jnp.dot(vector, working, precision=highest)  4.11 us
    unnamed x8, local copies, waits for them, and re-layouts  4.1 us
  transfers between devices with their start and end apart: 2, of which 2 were waited for; matrix products, arithmetic and copies ran while one was open for 0% of the time, Pallas kernels for 0%

profile of v2, /device:TPU:0, one launch (start us, length us, event | category | flops | bytes accessed | tf_op | source)
XLA Modules:
  0.0 189.5 jit_solution(406086770879196655)
XLA Ops:
  7.2 1.1 copy-done
  8.3 3.4 %fusion.8 = f32[72,32]{0,1:T(8,128)S(1)} fusion(f32[7168,32]{0,1:T(8,128)S(1)} %copy-done, bf16[1,72,7168]{2,1,0:T(8,128)(2,1)} %param.6, bf16[1,72,7168]{2,1,0:T(8,128)(2,1)} %param.5), kind=kOutput, calls=%fused_computation.13 | convolution fusion | flops 199729152 | bytes 2991104 | tf_op jit(solution)/shard_map/dot_general | solution.py:29
  11.7 42.1 %psum.7 = f32[72,32]{0,1:T(8,128)S(1)} all-reduce(f32[72,32]{0,1:T(8,128)S(1)} %fusion.8), channel_id=1, replica_groups=mesh['local'=4,'dp'=8] {'local','dp'}, use_global_device_ids=true, to_apply=%region_0.0 | all-reduce | flops 2304 | bytes 18432 | tf_op jit(solution)/shard_map/psum | solution.py:30
  53.8 51.1 %while.14 = (s32[]{:T(128)}, f32[72,32]{0,1:T(8,128)S(1)}, s32[]{:T(128)}, f32[]{:T(128)}, s32[]{:T(128)}) while((s32[]{:T(128)}, f32[72,32]{0,1:T(8,128)S(1)}, s32[]{:T(128)}, f32[]{:T(128)}, s32[]{:T(128)}) %tuple.35), condition=%wide.region_3.4_spmd.clone, body=%wide.region_1.3_spmd.clone.sunk | while | flops 32610 | bytes 30617 | solution.py:22
  55.4 0.6 multiply_reduce_fusion.2
  57.0 0.6 multiply_reduce_fusion.2
  58.6 0.6 multiply_reduce_fusion.2
  60.2 0.6 multiply_reduce_fusion.2
  65.0 0.6 multiply_reduce_fusion.2
  69.8 0.6 multiply_reduce_fusion.2
  76.2 0.6 multiply_reduce_fusion.2
  81.0 0.6 multiply_reduce_fusion.2
  85.8 0.6 multiply_reduce_fusion.2
  88.9 0.6 multiply_reduce_fusion.2
  92.1 0.6 multiply_reduce_fusion.2
  96.9 0.6 multiply_reduce_fusion.2
  103.3 0.6 multiply_reduce_fusion.2
  104.9 2.4 %fusion.6 = f32[7168,32]{0,1:T(8,128)} fusion(f32[72,32]{0,1:T(8,128)S(1)} %get-tuple-element.66, bf16[1,72,7168]{2,1,0:T(8,128)(2,1)S(1)} %copy-done.1, bf16[1,72,7168]{2,1,0:T(8,128)(2,1)S(1)} %copy-done.2), kind=kOutput, calls=%fused_computation.11 | convolution fusion | flops 199729152 | bytes 2991104 | tf_op jit(solution)/shard_map/dot_general | solution.py:32
  107.4 27.0 %reduce-scatter.2.cloned.1.call-done = f32[1792,32]{0,1:T(8,128)} async-done(((f32[7168,32]{0,1:T(8,128)}), f32[1792,32]{0,1:T(8,128)}) %reduce-scatter.2.cloned.1.call-update) | async-done | bytes 229392 | tf_op jit(solution)/shard_map/reduce_scatter | solution.py:33
  134.5 28.6 %all-gather.3.cloned.1.call-done = f32[14336,32]{0,1:T(8,128)} async-done(((f32[1792,32]{0,1:T(8,128)}), f32[14336,32]{0,1:T(8,128)}) %all-gather.3.cloned.1.call-update) | async-done | bytes 1835024 | tf_op jit(solution)/shard_map/all_gather | solution.py:34
  163.1 2.1 %copy.5 = f32[4,8,8,1792]{3,2,1,0:T(8,128)S(1)} copy(f32[4,8,8,1792]{3,1,2,0:T(8,128)} %bitcast.33) | data formatting | bytes 3670016
  165.6 13.2 %all_gather.11 = f32[7168,32]{0,1:T(8,128)S(1)} all-gather(f32[1792,32]{0,1:T(8,128)S(1)} %bitcast_reduce_fusion), channel_id=1, replica_groups=mesh['local'=4,'dp'=8] {'local'}, dimensions={0}, use_global_device_ids=true | all-gather | bytes 1146880 | tf_op jit(solution)/shard_map/all_gather | solution.py:35
  178.8 2.9 %fusion.5 = bf16[1,72,7168]{2,1,0:T(8,128)(2,1)} fusion(f32[72,32]{0,1:T(8,128)S(1)} %get-tuple-element.66, f32[7168,32]{0,1:T(8,128)S(1)} %all_gather.11, bf16[1,72,7168]{2,1,0:T(8,128)(2,1)S(1)} %copy-done.1, bf16[1,72,7168]{2,1,0:T(8,128)(2,1)S(1)} %copy-done.2), kind=kOutput, calls=%fused_computation.10 | convolution fusion | flops 201277440 | bytes 4023296 | tf_op jit(solution)/shard_map/dot_general | solution.py:36
  181.7 0.9 copy.14
  (189 shorter events, 20.5 us)
Async XLA Ops:
  7.2 1.2 copy-start
  7.2 97.7 %copy-start.1 = (bf16[1,72,7168]{2,1,0:T(8,128)(2,1)S(1)}, bf16[1,72,7168]{2,1,0:T(8,128)(2,1)}, u32[]{:S(2)}) copy-start(bf16[1,72,7168]{2,1,0:T(8,128)(2,1)} %param.6) | copy-start | bytes 3096580
  7.2 97.7 %copy-start.2 = (bf16[1,72,7168]{2,1,0:T(8,128)(2,1)S(1)}, bf16[1,72,7168]{2,1,0:T(8,128)(2,1)}, u32[]{:S(2)}) copy-start(bf16[1,72,7168]{2,1,0:T(8,128)(2,1)} %param.5) | copy-start | bytes 3096580
  7.2 127.3 %reduce-scatter.2.cloned.1.call-start = ((), (), s32[]{:S(2)}) async-start(), calls=%async_computation.1 | async-start | bytes 1146880 | tf_op jit(solution)/shard_map/reduce_scatter | solution.py:33
  107.4 55.7 %all-gather.3.cloned.1.call-start = ((), (), s32[]{:S(2)}) async-start(), calls=%async_computation.2 | async-start | bytes 2064384 | tf_op jit(solution)/shard_map/all_gather | solution.py:34
Sparse Core Ops, SparseCore 0:
  107.5 26.8 reduce-scatter.1
  136.1 26.9 all-gather.2
